TPU v7x, 32 devices: a whole 2x2x4 slice. The times are simulated.
32 devices in a mesh: smp: 8 (over z, y), var: 4 (over x, core).
Axes of the slice: x: 2, y: 2, z: 4, core: 2. Of those that a mesh axis runs over, the one named last changes fastest.
Arguments:
- dosage: int32 [512, 2048], P('smp', 'var'), may hold values from -2147483648 to 2147483647, as said below
- shares_init: float32 [12, 8192], P(None, ('smp', 'var')), may hold values from 0.1 to 1
- freqs_init: float32 [12, 2048], P(None, ('var', 'smp')), may hold values from 0.019 to 0.981
Outputs:
- shares: float32 [12, 8192], P(None, ('smp', 'var'))
- freqs: float32 [12, 2048], P(None, ('var', 'smp'))
Inputs may be any that keep to these rules, and one draw needn't show every extreme that they name: Every 2-bit code in a word of dosage is 0, 1, 2 or 3, and 3 marks a missing genotype.
All inputs are finite; a program needn't handle non-finite values.
Results may differ from a plain program's by a relative error of at most 0.0003.
Values sent between devices are 32-bit elements; how exact they have to be, the bound alone decides.
A program may use at most 64 MiB of HBM per device.

v0:
```python
import jax
import jax.numpy as jnp
from jax import lax
from jax.sharding import PartitionSpec as P

ITERS = 2
HIGH = lax.Precision.HIGHEST


def unpack_codes(packed):
    shifts = 2 * jnp.arange(16, dtype=jnp.int32)
    codes = jnp.bitwise_and(jnp.right_shift(packed[:, None, :], shifts[None, :, None]), 3)
    return codes.reshape(packed.shape[0] * 16, packed.shape[1])


def expect_sums(packed, shares_block, freqs_block):
    codes = unpack_codes(packed)
    live = (codes < 3).astype(jnp.float32)
    allele_f = live * codes.astype(jnp.float32)
    probs = jnp.einsum("kn,km->nm", shares_block, freqs_block, precision=HIGH)
    ratio_alt = allele_f / probs
    ratio_ref = (2.0 * live - allele_f) / (1.0 - probs)
    sum_q = jnp.einsum("km,nm->kn", freqs_block, ratio_alt, precision=HIGH) + jnp.einsum(
        "km,nm->kn", 1.0 - freqs_block, ratio_ref, precision=HIGH
    )
    sum_a = jnp.einsum("kn,nm->km", shares_block, ratio_alt, precision=HIGH)
    sum_b = jnp.einsum("kn,nm->km", shares_block, ratio_ref, precision=HIGH)
    return (sum_q, sum_a, sum_b)


def block_sums(packed, shares_block, freqs_block):
    word_rows = min(packed.shape[0], 16)
    blocks = packed.shape[0] // word_rows
    populations = shares_block.shape[0]
    packed_blocks = packed.reshape(blocks, word_rows, packed.shape[1])
    share_blocks = shares_block.reshape(populations, blocks, word_rows * 16).transpose(1, 0, 2)

    def one_block(carry, items):
        sum_q, sum_a, sum_b = expect_sums(items[0], items[1], freqs_block)
        return ((carry[0] + sum_a, carry[1] + sum_b), sum_q)

    start = (jnp.zeros(freqs_block.shape, jnp.float32), jnp.zeros(freqs_block.shape, jnp.float32))
    totals, sums_q = lax.scan(one_block, start, (packed_blocks, share_blocks))
    sum_q = sums_q.transpose(1, 0, 2).reshape(populations, shares_block.shape[1])
    return (sum_q, totals[0], totals[1])


def renew_shares(shares_block, sum_q):
    numer = shares_block * sum_q
    return (numer + 0.5) / (jnp.sum(numer, axis=0, keepdims=True) + 0.5 * shares_block.shape[0])


def renew_freqs(freqs_block, sum_a, sum_b):
    alt_part = freqs_block * sum_a
    ref_part = (1.0 - freqs_block) * sum_b
    return (alt_part + 0.5) / (alt_part + ref_part + 1.0)


def body(dosage, shares_init, freqs_init):
    own_shares = shares_init / jnp.sum(shares_init, axis=0, keepdims=True)
    own_freqs = freqs_init
    share_width = shares_init.shape[1]
    freq_width = freqs_init.shape[1]
    shares_block = lax.all_gather(own_shares, "var", axis=1, tiled=True)
    freqs_block = lax.all_gather(own_freqs, "smp", axis=1, tiled=True)
    for iteration in range(ITERS):
        part_q, part_a, part_b = block_sums(dosage, shares_block, freqs_block)
        sum_q = lax.psum(part_q, "var")
        sum_a, sum_b = lax.psum((part_a, part_b), "smp")
        shares_block = renew_shares(shares_block, sum_q)
        freqs_block = renew_freqs(freqs_block, sum_a, sum_b)
        if iteration + 1 == ITERS:
            own_shares = lax.dynamic_slice_in_dim(
                shares_block, lax.axis_index("var") * share_width, share_width, 1
            )
            own_freqs = lax.dynamic_slice_in_dim(
                freqs_block, lax.axis_index("smp") * freq_width, freq_width, 1
            )
    return (own_shares, own_freqs)


def solution(mesh):
    placed = (P("smp", "var"), P(None, ("smp", "var")), P(None, ("var", "smp")))
    return jax.shard_map(
        body,
        mesh=mesh,
        in_specs=placed,
        out_specs=(P(None, ("smp", "var")), P(None, ("var", "smp"))),
        check_vma=False,
    )
```

profile of v0, /device:TPU:0, one launch (start us, length us, event | category | flops | bytes accessed | tf_op | source)
XLA Modules:
  0.0 156.3 jit_solution(4070201371241163746)
XLA Ops:
  0.6 0.8 reduce_sum.27
  1.4 6.2 %all_gather.6 = f32[12,1024]{1,0:T(8,128)S(1)} all-gather(f32[12,256]{1,0:T(8,128)S(1)} %broadcast_divide_fusion), channel_id=1, replica_groups=mesh['smp'=8,'var'=4] {'var'}, dimensions={1}, use_global_device_ids=true | all-gather | bytes 61440 | tf_op jit(solution)/shard_map/all_gather | solution.py:64
  7.7 0.7 copy-done.2
  8.4 31.4 %all-gather = f32[8,64,12]{1,2,0:T(8,128)S(1)} all-gather(f32[1,64,12]{1,2,0:T(8,128)S(1)} %bitcast.171), channel_id=1, replica_groups=mesh['smp'=8,'var'=4] {'smp'}, dimensions={0}, use_global_device_ids=true | all-gather | bytes 27648 | tf_op jit(solution)/shard_map/all_gather | solution.py:65
  39.9 0.8 copy-done
  40.7 10.8 %while.30 = (s32[]{:T(128)}, f32[12,512]{1,0:T(8,128)S(1)}, f32[12,512]{1,0:T(8,128)S(1)}, f32[4,12,256]{2,1,0:T(8,128)S(1)}, f32[4,12,256]{2,1,0:T(8,128)S(1)},...) while((s32[]{:T(128)}, f32[12,512]{1,0:T(8,128)S(1)}, ...), condition=%wide.region_2.3_spmd.clone, body=%wide.region_1.2_spmd.clone.sunk | while | flops 95716368 | bytes 3547396 | solution.py:43
  40.8 0.8 fusion.92
  41.6 0.4 convolution_add_fusion.10
  41.9 0.4 convolution_add_fusion.11
  42.3 0.5 convolution_bitcast_fusion.4
  42.8 0.5 fusion.93
  43.5 0.8 fusion.92
  44.2 0.4 convolution_add_fusion.10
  44.6 0.4 convolution_add_fusion.11
  45.0 0.5 convolution_bitcast_fusion.4
  45.5 0.5 fusion.93
  46.2 0.8 fusion.92
  46.9 0.4 convolution_add_fusion.10
  47.3 0.4 convolution_add_fusion.11
  47.7 0.5 convolution_bitcast_fusion.4
  48.2 0.5 fusion.93
  48.8 0.8 fusion.92
  49.6 0.4 convolution_add_fusion.10
  50.4 0.5 convolution_bitcast_fusion.4
  50.9 0.5 fusion.93
  51.5 10.7 %psum.42 = f32[12,1024]{1,0:T(8,128)S(1)} all-reduce(f32[12,1024]{1,0:T(8,128)S(1)} %bitcast.169), channel_id=1, replica_groups=mesh['smp'=8,'var'=4] {'var'}, use_global_device_ids=true, to_apply=%region_3.4 | all-reduce | flops 12288 | bytes 98304 | tf_op jit(solution)/shard_map/psum | solution.py:68
  62.3 37.5 %all-reduce.1 = (f32[12,512]{1,0:T(8,128)S(1)}, f32[12,512]{1,0:T(8,128)S(1)}) all-reduce(f32[12,512]{1,0:T(8,128)S(1)} %get-tuple-element.82, f32[12,512]{1,0:T(8,128)S(1)} %get-tuple-element.81), channel_id=1, replica_groups=mesh['smp'=8,'var'=4] {'smp'}, use_global_device_ids=true, to_apply=%region_6.7 | all-reduce | flops 12288 | bytes 98304 | tf_op jit(solution)/shard_map/psum | solution.py:69
  99.9 10.8 %while.31 = (s32[]{:T(128)}, f32[12,512]{1,0:T(8,128)S(1)}, f32[12,512]{1,0:T(8,128)S(1)}, f32[4,12,256]{2,1,0:T(8,128)S(1)}, f32[4,12,256]{2,1,0:T(8,128)S(1)},...) while((s32[]{:T(128)}, f32[12,512]{1,0:T(8,128)S(1)}, ...), condition=%wide.region_8.9_spmd.clone, body=%wide.region_7.8_spmd.clone.sunk | while | flops 95716368 | bytes 3547396 | solution.py:43
  100.0 0.8 fusion.103
  100.8 0.4 convolution_add_fusion.12
  101.5 0.5 convolution_bitcast_fusion.5
  102.1 0.5 fusion.104
  102.7 0.8 fusion.103
  103.5 0.4 convolution_add_fusion.12
  104.2 0.5 convolution_bitcast_fusion.5
  104.8 0.5 fusion.104
  105.4 0.8 fusion.103
  106.2 0.4 convolution_add_fusion.12
  106.9 0.5 convolution_bitcast_fusion.5
  107.5 0.5 fusion.104
  108.1 0.8 fusion.103
  108.9 0.4 convolution_add_fusion.12
  109.6 0.5 convolution_bitcast_fusion.5
  110.2 0.5 fusion.104
  110.8 10.7 %psum.45 = f32[12,1024]{1,0:T(8,128)S(1)} all-reduce(f32[12,1024]{1,0:T(8,128)S(1)} %bitcast.170), channel_id=1, replica_groups=mesh['smp'=8,'var'=4] {'var'}, use_global_device_ids=true, to_apply=%region_9.10 | all-reduce | flops 12288 | bytes 98304 | tf_op jit(solution)/shard_map/psum | solution.py:68
  121.6 0.6 fusion.44
  122.2 33.4 %all-reduce = (f32[12,512]{1,0:T(8,128)S(1)}, f32[12,512]{1,0:T(8,128)S(1)}) all-reduce(f32[12,512]{1,0:T(8,128)S(1)} %get-tuple-element.85, f32[12,512]{1,0:T(8,128)S(1)} %get-tuple-element.84), channel_id=1, replica_groups=mesh['smp'=8,'var'=4] {'smp'}, use_global_device_ids=true, to_apply=%region_12.13 | all-reduce | flops 12288 | bytes 98304 | tf_op jit(solution)/shard_map/psum | solution.py:69
  155.6 0.7 fusion.47
  (67 shorter events, 3.1 us)
Async XLA Ops:
  0.6 0.8 copy-start.1
  7.7 0.7 copy-start.2
  39.8 0.9 copy-start
where the time goes:
time: 157 us; the launch traced here: 156 us
  blocking collectives  130 us (83%)
  matrix products  20.5 us (13%)
  local copies, waits for them, and re-layouts  2.55 us (2%)
  other arithmetic  2.3 us (1%)
    psum x2, blocking collectives, body(): sum_a, sum_b = lax.psum((part_a, part_b), 'smp')  70.9 us
    all_gather x1, blocking collectives, body(): freqs_block = lax.all_gather(own_freqs, 'smp', axis=1, tiled=True)  31.4 us
    psum x2, blocking collectives, body(): sum_q = lax.psum(part_q, 'var')  21.3 us
    dot_general x8, matrix products, expect_sums(): probs = jnp.einsum('kn,km->nm', shares_block, freqs_block, precision=HIGH)  6.22 us
    all_gather x1, blocking collectives, body(): shares_block = lax.all_gather(own_shares, 'var', axis=1, tiled=True)  6.22 us
    dot_general x8, matrix products, expect_sums(): jnp.einsum('km,nm->kn', 1.0 - freqs_block, ratio_ref, precision=HIGH)  4.22 us
    dot_general x8, matrix products, expect_sums(): jnp.einsum('km,nm->kn', freqs_block, ratio_alt, precision=HIGH)  4.14 us

commit v1 on v0

--- a/solution.py
+++ b/solution.py
@@ -2,6 +2,7 @@
 import jax.numpy as jnp
 from jax import lax
 from jax.sharding import PartitionSpec as P
+from jax.lax import all_gather
 
 ITERS = 2
 HIGH = lax.Precision.HIGHEST
@@ -65,7 +66,8 @@
     freqs_block = lax.all_gather(own_freqs, "smp", axis=1, tiled=True)
     for iteration in range(ITERS):
         part_q, part_a, part_b = block_sums(dosage, shares_block, freqs_block)
-        sum_q = lax.psum(part_q, "var")
+        end_streams_on_mesh = lambda chunk: jnp.sum(all_gather(chunk, axis_name="var"), axis=0)
+        sum_q = end_streams_on_mesh(part_q)
         sum_a, sum_b = lax.psum((part_a, part_b), "smp")
         shares_block = renew_shares(shares_block, sum_q)
         freqs_block = renew_freqs(freqs_block, sum_a, sum_b)

time: 157 us -> 147 us (0.936)
  blocking collectives: 130 us -> 120 us
    psum x2 -> x0, blocking collectives: 21.3 us -> none  [body(): sum_q = lax.psum(part_q, 'var')]
    all_gather x0 -> x2, blocking collectives: none -> 11.6 us  [body(): all_gather(chunk, axis_name='var')]
where the time goes in v1:
time: 147 us
  blocking collectives  120 us (82%)
  matrix products  20.5 us (14%)
  local copies, waits for them, and re-layouts  2.55 us (2%)
  other arithmetic  2.33 us (2%)
    psum x2, blocking collectives, body(): sum_a, sum_b = lax.psum((part_a, part_b), 'smp')  70.9 us
    all_gather x1, blocking collectives, body(): freqs_block = lax.all_gather(own_freqs, 'smp', axis=1, tiled=True)  31.4 us
    all_gather x2, blocking collectives, body(): all_gather(chunk, axis_name='var')  11.6 us
    dot_general x8, matrix products, expect_sums(): probs = jnp.einsum('kn,km->nm', shares_block, freqs_block, precision=HIGH)  6.22 us
    all_gather x1, blocking collectives, body(): shares_block = lax.all_gather(own_shares, 'var', axis=1, tiled=True)  6.22 us
    dot_general x8, matrix products, expect_sums(): jnp.einsum('km,nm->kn', 1.0 - freqs_block, ratio_ref, precision=HIGH)  4.22 us
    dot_general x8, matrix products, expect_sums(): jnp.einsum('km,nm->kn', freqs_block, ratio_alt, precision=HIGH)  4.14 us
    dot_general x8, matrix products, expect_sums(): sum_a = jnp.einsum('kn,nm->km', shares_block, ratio_alt, precision=HIGH)  2.96 us

profile of v1, /device:TPU:0, one launch (start us, length us, event | category | flops | bytes accessed | tf_op | source)
XLA Modules:
  0.0 146.5 jit_solution(7675783077697571270)
XLA Ops:
  0.6 0.8 reduce_sum.45
  1.4 6.2 %all_gather.12 = f32[12,1024]{1,0:T(8,128)S(1)} all-gather(f32[12,256]{1,0:T(8,128)S(1)} %broadcast_divide_fusion), channel_id=1, replica_groups=mesh['smp'=8,'var'=4] {'var'}, dimensions={1}, use_global_device_ids=true | all-gather | bytes 61440 | tf_op jit(solution)/shard_map/all_gather | solution.py:65
  7.7 0.7 copy-done.2
  8.4 31.4 %all-gather = f32[8,64,12]{1,2,0:T(8,128)S(1)} all-gather(f32[1,64,12]{1,2,0:T(8,128)S(1)} %bitcast.161), channel_id=1, replica_groups=mesh['smp'=8,'var'=4] {'smp'}, dimensions={0}, use_global_device_ids=true | all-gather | bytes 27648 | tf_op jit(solution)/shard_map/all_gather | solution.py:66
  39.9 0.8 copy-done
  40.7 10.8 %while.30 = (s32[]{:T(128)}, f32[12,512]{1,0:T(8,128)S(1)}, f32[12,512]{1,0:T(8,128)S(1)}, f32[4,12,256]{2,1,0:T(8,128)S(1)}, f32[4,12,256]{2,1,0:T(8,128)S(1)},...) while((s32[]{:T(128)}, f32[12,512]{1,0:T(8,128)S(1)}, ...), condition=%wide.region_2.3_spmd.clone, body=%wide.region_1.2_spmd.clone.sunk | while | flops 95716368 | bytes 3547396 | solution.py:44
  40.8 0.8 fusion.92
  41.6 0.4 convolution_add_fusion.10
  41.9 0.4 convolution_add_fusion.11
  42.3 0.5 convolution_bitcast_fusion.4
  42.8 0.5 fusion.93
  43.5 0.8 fusion.92
  44.2 0.4 convolution_add_fusion.10
  44.6 0.4 convolution_add_fusion.11
  45.0 0.5 convolution_bitcast_fusion.4
  45.5 0.5 fusion.93
  46.2 0.8 fusion.92
  46.9 0.4 convolution_add_fusion.10
  47.3 0.4 convolution_add_fusion.11
  47.7 0.5 convolution_bitcast_fusion.4
  48.2 0.5 fusion.93
  48.8 0.8 fusion.92
  49.6 0.4 convolution_add_fusion.10
  50.4 0.5 convolution_bitcast_fusion.4
  50.9 0.5 fusion.93
  51.5 5.8 %all_gather.14 = f32[4,12,1024]{2,1,0:T(8,128)S(1)} all-gather(f32[1,12,1024]{2,1,0:T(8,128)S(1)} %all_gather_reshape.6), channel_id=1, replica_groups=mesh['smp'=8,'var'=4] {'var'}, dimensions={0}, use_global_device_ids=true | all-gather | bytes 245760 | tf_op jit(solution)/shard_map/all_gather | solution.py:69
  57.4 37.5 %all-reduce.1 = (f32[12,512]{1,0:T(8,128)S(1)}, f32[12,512]{1,0:T(8,128)S(1)}) all-reduce(f32[12,512]{1,0:T(8,128)S(1)} %get-tuple-element.82, f32[12,512]{1,0:T(8,128)S(1)} %get-tuple-element.81), channel_id=1, replica_groups=mesh['smp'=8,'var'=4] {'smp'}, use_global_device_ids=true, to_apply=%region_6.7 | all-reduce | flops 12288 | bytes 98304 | tf_op jit(solution)/shard_map/psum | solution.py:71
  95.0 10.8 %while.31 = (s32[]{:T(128)}, f32[12,512]{1,0:T(8,128)S(1)}, f32[12,512]{1,0:T(8,128)S(1)}, f32[4,12,256]{2,1,0:T(8,128)S(1)}, f32[4,12,256]{2,1,0:T(8,128)S(1)},...) while((s32[]{:T(128)}, f32[12,512]{1,0:T(8,128)S(1)}, ...), condition=%wide.region_8.9_spmd.clone, body=%wide.region_7.8_spmd.clone.sunk | while | flops 95716368 | bytes 3547396 | solution.py:44
  95.1 0.8 fusion.103
  95.9 0.4 convolution_add_fusion.12
  96.7 0.5 convolution_bitcast_fusion.5
  97.2 0.5 fusion.104
  97.8 0.8 fusion.103
  98.6 0.4 convolution_add_fusion.12
  99.4 0.5 convolution_bitcast_fusion.5
  99.9 0.5 fusion.104
  100.5 0.8 fusion.103
  101.3 0.4 convolution_add_fusion.12
  102.1 0.5 convolution_bitcast_fusion.5
  102.6 0.5 fusion.104
  103.2 0.8 fusion.103
  104.0 0.4 convolution_add_fusion.12
  104.7 0.5 convolution_bitcast_fusion.5
  105.3 0.5 fusion.104
  105.9 5.8 %all_gather.15 = f32[4,12,1024]{2,1,0:T(8,128)S(1)} all-gather(f32[1,12,1024]{2,1,0:T(8,128)S(1)} %all_gather_reshape.7), channel_id=1, replica_groups=mesh['smp'=8,'var'=4] {'var'}, dimensions={0}, use_global_device_ids=true | all-gather | bytes 245760 | tf_op jit(solution)/shard_map/all_gather | solution.py:69
  111.8 0.6 fusion.44
  112.4 33.4 %all-reduce = (f32[12,512]{1,0:T(8,128)S(1)}, f32[12,512]{1,0:T(8,128)S(1)}) all-reduce(f32[12,512]{1,0:T(8,128)S(1)} %get-tuple-element.85, f32[12,512]{1,0:T(8,128)S(1)} %get-tuple-element.84), channel_id=1, replica_groups=mesh['smp'=8,'var'=4] {'smp'}, use_global_device_ids=true, to_apply=%region_12.13 | all-reduce | flops 12288 | bytes 98304 | tf_op jit(solution)/shard_map/psum | solution.py:71
  145.8 0.7 fusion.47
  (67 shorter events, 3.2 us)
Async XLA Ops:
  0.6 0.8 copy-start.1
  7.7 0.7 copy-start.2
  39.8 0.9 copy-start
